TPU v7x, 128 devices: a whole 4x4x4 slice. The times are simulated.
128 devices in a mesh: rep: 1, r: 4 (over x), s: 32 (over y, z, core).
Axes of the slice: x: 4, y: 4, z: 4, core: 2. Of those that a mesh axis runs over, the one named last changes fastest.
Arguments:
- x: bfloat16 [128, 2048, 1280], P(('rep', 'r', 's'))
- dy: bfloat16 [128, 2048, 1280], P(('rep', 'r', 's'))
- w_gate: bfloat16 [2, 1280, 4480], P(None, 's')
- w_up: bfloat16 [2, 1280, 4480], P(None, 's')
- w_down: bfloat16 [2, 4480, 1280], P(None, 's')
Outputs:
- output 1: bfloat16 [128, 2048, 1280], P(('rep', 'r', 's'))
- output 2: bfloat16 [2, 1280, 4480], P('rep', 's')
- output 3: bfloat16 [2, 1280, 4480], P('rep', 's')
- output 4: bfloat16 [2, 4480, 1280], P('rep', 's')
All inputs are finite; a program needn't handle non-finite values.
Results may differ from a plain program's by a relative error of at most 0.018.
Values are sent between devices in bfloat16 or wider.
A program may use at most 1.5 GiB of HBM per device.

v0:
```python
import jax
import jax.numpy as jnp
from jax import lax
from jax.sharding import PartitionSpec as P

NAMES = ("w_gate", "w_up", "w_down")


def matmul(a, w):
    return jnp.dot(a, w, preferred_element_type=jnp.float32).astype(jnp.bfloat16)


def normed(h):
    wide = h.astype(jnp.float32)
    scale = lax.rsqrt(jnp.mean(wide**2, -1, keepdims=True) + 1e-6)
    return (wide * scale).astype(jnp.bfloat16)


def layer(h, w):
    a = normed(h)
    gate = jnp.dot(a, w["w_gate"], preferred_element_type=jnp.float32)
    up = jnp.dot(a, w["w_up"], preferred_element_type=jnp.float32)
    return h + matmul((jax.nn.silu(gate) * up).astype(jnp.bfloat16), w["w_down"])


def solution(mesh):
    def fetched(weights, number):
        return {name: lax.all_gather(w[number], "s", axis=0, tiled=True) for name, w in zip(NAMES, weights, strict=True)}

    def summed(term):
        return lax.psum(lax.psum_scatter(term, "s", scatter_dimension=0, tiled=True), "r")

    def step(x, dy, *weights):
        layers = weights[0].shape[0]
        h, inputs = x[0], []
        for number in range(layers):
            inputs.append(h)
            h = layer(h, fetched(weights, number))
        by_h, mine = dy[0], [None] * layers
        for number in reversed(range(layers)):
            _, back = jax.vjp(lambda w, h: layer(h, w), fetched(weights, number), inputs[number])
            by_w, by_h = back(by_h)
            mine[number] = [summed(by_w[name]) for name in NAMES]
        return (by_h[None], *(jnp.stack([mine[number][i] for number in range(layers)]) for i in range(3)))

    states, cut = P(("rep", "r", "s"), None, None), P(None, "s", None)
    return jax.shard_map(
        step,
        mesh=mesh,
        in_specs=(states, states) + (cut,) * 3,
        out_specs=(states,) + (P("rep", "s", None),) * 3,
        check_vma=False,
    )
```

profile of v0, /device:TPU:1, one launch (start us, length us, event | category | flops | bytes accessed | tf_op | source)
XLA Modules:
  0.0 1333.0 jit_solution(11404643588190619133)
XLA Ops:
  7.2 2.0 fusion.90
  9.3 2.0 fusion.92
  11.4 3.7 fusion.91
  17.0 7.9 copy.20
  24.8 3.6 fusion.37
  28.4 0.6 copy-done
  29.0 8.0 copy.19
  37.0 36.7 %all-gather.13.cloned.1.call-done = bf16[1,1280,4480]{2,1,0:T(8,128)(2,1)} async-done(((bf16[1,40,4480]{2,1,0:T(8,128)(2,1)}), bf16[1,1280,4480]{2,1,0:T(8,128)(2,1)}) %all-gather.13.cloned.1.call-update) | async-done | bytes 11468816 | tf_op jit(solution)/shard_map/all_gather | solution.py:28
  73.7 32.1 %fusion.31 = f32[2048,4480]{1,0:T(8,128)} fusion(bf16[1,1280,4480]{2,1,0:T(8,128)(2,1)} %all-gather.13.cloned.1.call-done, bf16[1,2048,1280]{1,2,0:T(8,128)(2,1)} %copy.20, f32[2048]{0:T(1024)S(1)} %fusion.82), kind=kOutput, calls=%fused_computation.55 | convolution fusion | flops 23495966720 | bytes 53420032 | tf_op jit(solution)/shard_map/dot_general | solution.py:21
  105.8 29.5 %all-gather.15.cloned.1.call-done = bf16[1,1280,4480]{2,1,0:T(8,128)(2,1)} async-done(((bf16[1,40,4480]{2,1,0:T(8,128)(2,1)}), bf16[1,1280,4480]{2,1,0:T(8,128)(2,1)}) %all-gather.15.cloned.1.call-update) | async-done | bytes 11468816 | tf_op jit(solution)/shard_map/all_gather | solution.py:28
  135.3 45.3 %multiply_convert_fusion.1 = (bf16[2048,4480]{1,0:T(8,128)(2,1)}, f32[2048,4480]{1,0:T(8,128)}) fusion(f32[2048,4480]{1,0:T(8,128)} %fusion.31, bf16[1,1280,4480]{2,1,0:T(8,128)(2,1)} %all-gather.15.cloned.1.call-done, bf16[1,2048,1280]{1,2,0:T(8,128)(2,1)} %copy.20, f32[2048]{0:T(1024)S(1)} %fusion.82), kind=kOutput, calls=%fused_computation.13 | convolution fusion | flops 23551016960 | bytes 108470272 | tf_op jit(solution)/shard_map/dot_general | solution.py:22
  180.6 43.7 %all-gather.17.cloned.1.call-done = bf16[1,4480,1280]{2,0,1:T(2,128)(2,1)} async-done(((bf16[1,140,1280]{2,0,1:T(2,128)(2,1)}), bf16[1,4480,1280]{2,0,1:T(2,128)(2,1)}) %all-gather.17.cloned.1.call-update) | async-done | bytes 11468816 | tf_op jit(solution)/shard_map/all_gather | solution.py:28
  224.3 46.4 %fusion.40 = (f32[2048]{0:T(1024)S(1)}, bf16[2048,1280]{0,1:T(8,128)(2,1)}) fusion(bf16[2048,4480]{1,0:T(8,128)(2,1)} %get-tuple-element.32, bf16[1,4480,1280]{2,0,1:T(2,128)(2,1)} %all-gather.17.cloned.1.call-done, bf16[1,2048,1280]{1,2,0:T(8,128)(2,1)} %copy.20), kind=kOutput, calls=%fused_computation.64 | convolution fusion | flops 23501207552 | bytes 40312832 | tf_op jit(solution)/shard_map/dot_general | solution.py:10
  270.7 42.3 %all-gather.21.cloned.1.call-done = bf16[1,4480,1280]{2,0,1:T(2,128)(2,1)} async-done(((bf16[1,140,1280]{2,0,1:T(2,128)(2,1)}), bf16[1,4480,1280]{2,0,1:T(2,128)(2,1)}) %all-gather.21.cloned.1.call-update) | async-done | bytes 11468816 | tf_op jit(solution)/shard_map/all_gather | solution.py:28
  313.0 33.1 %convolution_convert_fusion.1 = bf16[2048,4480]{1,0:T(8,128)(2,1)} fusion(bf16[1,4480,1280]{2,0,1:T(2,128)(2,1)} %all-gather.21.cloned.1.call-done, bf16[1,2048,1280]{2,1,0:T(8,128)(2,1)} %param.6), kind=kOutput, calls=%fused_computation.23 | convolution fusion | flops 23497277440 | bytes 35061760 | tf_op jit(solution)/shard_map/transpose(jvp())/dot_general | solution.py:10
  346.1 28.2 %all-gather.23.cloned.1.call-done = bf16[1,1280,4480]{2,1,0:T(8,128)(2,1)} async-done(((bf16[1,40,4480]{2,1,0:T(8,128)(2,1)}), bf16[1,1280,4480]{2,1,0:T(8,128)(2,1)}) %all-gather.23.cloned.1.call-update) | async-done | bytes 11468816 | tf_op jit(solution)/shard_map/all_gather | solution.py:28
  374.3 32.1 %fusion.19 = f32[2048,4480]{1,0:T(8,128)} fusion(bf16[1,1280,4480]{2,1,0:T(8,128)(2,1)} %all-gather.23.cloned.1.call-done, bf16[2048,1280]{0,1:T(8,128)(2,1)} %get-tuple-element.35, f32[2048]{0:T(1024)S(1)} %fusion.83), kind=kOutput, calls=%fused_computation.43 | convolution fusion | flops 23495966720 | bytes 53420032 | tf_op jit(solution)/shard_map/jvp()/dot_general | solution.py:22
  406.5 29.9 %all-gather.19.cloned.1.call-done = bf16[1,1280,4480]{2,1,0:T(8,128)(2,1)} async-done(((bf16[1,40,4480]{2,1,0:T(8,128)(2,1)}), bf16[1,1280,4480]{2,1,0:T(8,128)(2,1)}) %all-gather.19.cloned.1.call-update) | async-done | bytes 11468816 | tf_op jit(solution)/shard_map/all_gather | solution.py:28
  436.3 54.1 %fusion.3 = (bf16[2048,4480]{1,0:T(8,128)(2,1)}, f32[2048,4480]{1,0:T(8,128)}) fusion(f32[2048,4480]{1,0:T(8,128)} %fusion.19, bf16[2048,4480]{1,0:T(8,128)(2,1)} %convolution_convert_fusion.1, bf16[1,1280,4480]{2,1,0:T(8,128)(2,1)} %all-gather.19.cloned.1.call-done, bf16[2048,1280]{0,1:T(8,128)(2,1)} %get-tuple-element.35, f32[2048]{0:T(1024)S(1)} %fusion.83), kind=kOutput, calls=%fused_computation.7 | convolution fusion | flops 23606067200 | bytes 126820352 | tf_op jit(solution)/shard_map/jvp()/dot_general | solution.py:21
  490.4 35.3 %fusion.52 = bf16[2048,1280]{0,1:T(8,128)(2,1)} fusion(bf16[1,1280,4480]{2,1,0:T(8,128)(2,1)} %all-gather.23.cloned.1.call-done, bf16[2048,4480]{1,0:T(8,128)(2,1)} %convolution_convert_fusion.1, f32[2048,4480]{1,0:T(8,128)} %get-tuple-element.37), kind=kOutput, calls=%fused_computation.70 | convolution fusion | flops 23545774080 | bytes 71761920 | tf_op jit(solution)/shard_map/transpose(jvp())/dot_general | solution.py:22
  525.7 34.4 %fusion.42 = (f32[2048]{0:T(1024)S(1)}, bf16[2048,1280]{0,1:T(8,128)(2,1)}) fusion(bf16[2048,1280]{0,1:T(8,128)(2,1)} %get-tuple-element.35, bf16[2048,1280]{0,1:T(8,128)(2,1)} %fusion.52, bf16[2048,4480]{1,0:T(8,128)(2,1)} %get-tuple-element.36, bf16[1,1280,4480]{2,1,0:T(8,128)(2,1)} %all-gather.19.cloned.1.call-done), kind=kOutput, calls=%fused_computation.66 | convolution fusion | flops 23501207552 | bytes 45555712 | tf_op jit(solution)/shard_map/transpose(jvp())/dot_general | solution.py:21
  560.2 12.3 fusion.69
  572.5 54.4 %fusion.5 = (bf16[2048,4480]{1,0:T(8,128)(2,1)}, bf16[2048,4480]{1,0:T(8,128)(2,1)}) fusion(f32[2048,4480]{1,0:T(8,128)} %fusion.31, f32[2048,4480]{1,0:T(8,128)} %get-tuple-element.33, bf16[2048,1280]{0,1:T(8,128)(2,1)} %fusion.69, bf16[1,4480,1280]{2,0,1:T(2,128)(2,1)} %all-gather.17.cloned.1.call-done), kind=kOutput, calls=%fused_computation.9 | convolution fusion | flops 23607377920 | bytes 126812160 | tf_op jit(solution)/shard_map/transpose(jvp())/dot_general | solution.py:10
  627.0 37.6 %fusion.12 = bf16[1280,4480]{1,0:T(8,128)(2,1)} fusion(bf16[2048,4480]{1,0:T(8,128)(2,1)} %get-tuple-element.41, bf16[1,2048,1280]{1,2,0:T(8,128)(2,1)} %copy.20, f32[2048]{0:T(1024)S(1)} %copy-done.3, f32[2048,4480]{1,0:T(8,128)} %fusion.31), kind=kOutput, calls=%fused_computation.20 | convolution fusion | flops 23556751360 | bytes 71770112 | tf_op jit(solution)/shard_map/transpose(jvp())/dot_general | solution.py:22
  664.7 0.6 copy-done.7
  665.3 37.3 %fusion.13 = bf16[1280,4480]{1,0:T(8,128)(2,1)} fusion(bf16[2048,4480]{1,0:T(8,128)(2,1)} %convolution_convert_fusion.1, bf16[2048,1280]{0,1:T(8,128)(2,1)} %get-tuple-element.35, f32[2048]{0:T(1024)S(1)} %copy-done.7, f32[2048,4480]{1,0:T(8,128)} %get-tuple-element.37), kind=kOutput, calls=%fused_computation.21 | convolution fusion | flops 23556751360 | bytes 71770112 | tf_op jit(solution)/shard_map/transpose(jvp())/dot_general | solution.py:22
  702.7 31.6 %convolution_convert_fusion.4 = bf16[1280,4480]{1,0:T(8,128)(2,1)} fusion(bf16[2048,4480]{1,0:T(8,128)(2,1)} %get-tuple-element.36, bf16[2048,1280]{0,1:T(8,128)(2,1)} %get-tuple-element.35, f32[2048]{0:T(1024)S(1)} %copy-done.7), kind=kOutput, calls=%fused_computation.26 | convolution fusion | flops 23495966720 | bytes 35069952 | tf_op jit(solution)/shard_map/transpose(jvp())/dot_general | solution.py:21
  735.0 0.6 dynamic-slice.14
  736.2 31.2 %convolution_convert_fusion.5 = bf16[1280,4480]{1,0:T(8,128)(2,1)} fusion(bf16[2048,4480]{1,0:T(8,128)(2,1)} %get-tuple-element.40, bf16[1,2048,1280]{1,2,0:T(8,128)(2,1)} %copy.20, f32[2048]{0:T(1024)S(1)} %copy-done.4), kind=kOutput, calls=%fused_computation.27 | convolution fusion | flops 23495966720 | bytes 35069952 | tf_op jit(solution)/shard_map/transpose(jvp())/dot_general | solution.py:21
  767.5 38.8 %convolution_convert_fusion.2 = bf16[4480,1280]{1,0:T(8,128)(2,1)} fusion(f32[2048,4480]{1,0:T(8,128)} %fusion.19, bf16[1,2048,1280]{2,1,0:T(8,128)(2,1)} %param.6, f32[2048,4480]{1,0:T(8,128)} %get-tuple-element.37), kind=kOutput, calls=%fused_computation.24 | convolution fusion | flops 23548887040 | bytes 90112000 | tf_op jit(solution)/shard_map/transpose(jvp())/dot_general | solution.py:10
  806.4 29.9 %convolution_convert_fusion.3 = bf16[4480,1280]{1,0:T(8,128)(2,1)} fusion(bf16[2048,4480]{1,0:T(8,128)(2,1)} %get-tuple-element.32, bf16[2048,1280]{0,1:T(8,128)(2,1)} %fusion.69), kind=kOutput, calls=%fused_computation.25 | convolution fusion | flops 23493836800 | bytes 35061760 | tf_op jit(solution)/shard_map/transpose(jvp())/dot_general | solution.py:10
  836.3 151.3 %fusion.89 = (bf16[144,1280]{1,0:T(8,128)(2,1)S(1)}, bf16[144,1280]{1,0:T(8,128)(2,1)S(1)}) fusion(bf16[4480,1280]{1,0:T(8,128)(2,1)} %convolution_convert_fusion.2, bf16[4480,1280]{1,0:T(8,128)(2,1)} %convolution_convert_fusion.3), kind=kCustom, calls=%all-reduce-scatter.2 | all-reduce-scatter fusion | flops 11796481 | bytes 23675392
  987.7 4.4 collective-permute-start
  992.2 1.9 collective-permute-start.1
  994.1 35.3 %fusion.49 = bf16[2048,1280]{0,1:T(8,128)(2,1)} fusion(bf16[1,1280,4480]{2,1,0:T(8,128)(2,1)} %all-gather.15.cloned.1.call-done, bf16[2048,4480]{1,0:T(8,128)(2,1)} %get-tuple-element.41, f32[2048,4480]{1,0:T(8,128)} %fusion.31), kind=kOutput, calls=%fused_computation.69 | convolution fusion | flops 23545774080 | bytes 71761920 | tf_op jit(solution)/shard_map/transpose(jvp())/dot_general | solution.py:22
  1029.4 1.2 concatenate
  1030.6 1.3 concatenate.1
  1031.9 0.8 dynamic-slice_bitcast_fusion.1
  1032.7 0.8 dynamic-slice_bitcast_fusion
  1033.6 104.1 %reduce-scatter.19.cloned.1.call-done = bf16[40,4480]{1,0:T(8,128)(2,1)} async-done(((bf16[1280,4480]{1,0:T(8,128)(2,1)}), bf16[40,4480]{1,0:T(8,128)(2,1)}) %reduce-scatter.19.cloned.1.call-update) | async-done | bytes 358416
  1137.7 119.2 %reduce-scatter.17.cloned.1.call-done = bf16[40,4480]{1,0:T(8,128)(2,1)} async-done(((bf16[1280,4480]{1,0:T(8,128)(2,1)}), bf16[40,4480]{1,0:T(8,128)(2,1)}) %reduce-scatter.17.cloned.1.call-update) | async-done | bytes 358416
  1257.0 34.3 %fusion.39 = (f32[2048]{0:T(1024)S(1)}, bf16[2048,1280]{0,1:T(8,128)(2,1)}) fusion(bf16[1,2048,1280]{1,2,0:T(8,128)(2,1)} %copy.20, bf16[2048,1280]{0,1:T(8,128)(2,1)} %fusion.49, bf16[2048,4480]{1,0:T(8,128)(2,1)} %get-tuple-element.40, bf16[1,1280,4480]{2,1,0:T(8,128)(2,1)} %all-gather.13.cloned.1.call-done), kind=kOutput, calls=%fused_computation.63 | convolution fusion | flops 23501207552 | bytes 45555712 | tf_op jit(solution)/shard_map/transpose(jvp())/dot_general | solution.py:21
  1291.3 12.3 fusion.68
  1303.7 7.9 copy.21
  1311.5 9.4 all-reduce.12.cloned.1.call-done
  1320.9 1.2 pad_maximum_fusion
  1322.1 1.4 copy.22
  1323.5 2.6 pad_maximum_fusion.1
  (52 shorter events, 3.0 us)
Async XLA Ops:
  7.2 66.5 %all-gather.13.cloned.1.call-start = ((), (), s32[]{:S(2)}) async-start(), calls=%async_computation.4 | async-start | bytes 11827200 | tf_op jit(solution)/shard_map/all_gather | solution.py:28
  9.2 126.0 %all-gather.15.cloned.1.call-start = ((), (), s32[]{:S(2)}) async-start(), calls=%async_computation.5 | async-start | bytes 11827200 | tf_op jit(solution)/shard_map/all_gather | solution.py:28
  11.4 212.9 %all-gather.17.cloned.1.call-start = ((), (), s32[]{:S(2)}) async-start(), calls=%async_computation.6 | async-start | bytes 23654400 | tf_op jit(solution)/shard_map/all_gather | solution.py:28
  15.2 297.9 %all-gather.21.cloned.1.call-start = ((), (), s32[]{:S(2)}) async-start(), calls=%async_computation.8 | async-start | bytes 23654400 | tf_op jit(solution)/shard_map/all_gather | solution.py:28
  15.7 358.6 %all-gather.23.cloned.1.call-start = ((), (), s32[]{:S(2)}) async-start(), calls=%async_computation.9 | async-start | bytes 11827200 | tf_op jit(solution)/shard_map/all_gather | solution.py:28
  16.3 420.0 %all-gather.19.cloned.1.call-start = ((), (), s32[]{:S(2)}) async-start(), calls=%async_computation.7 | async-start | bytes 11827200 | tf_op jit(solution)/shard_map/all_gather | solution.py:28
  16.9 1016.7 %reduce-scatter.21.cloned.1.call-start = ((), (), s32[]{:S(2)}) async-start(), calls=%async_computation.12 | async-start | bytes 11827200
  28.4 0.6 copy-start
  29.0 106.3 %copy-start.2 = (f32[2048]{0:T(1024)}, f32[2048]{0:T(1024)S(1)}, u32[]{:S(2)}) copy-start(f32[2048]{0:T(1024)S(1)} %fusion.82) | copy-start | bytes 24580
  270.7 75.4 %copy-start.8 = (f32[2048]{0:T(1024)}, f32[2048]{0:T(1024)S(1)}, u32[]{:S(2)}) copy-start(f32[2048]{0:T(1024)S(1)} %get-tuple-element.34) | copy-start | bytes 24580
  270.7 289.5 %copy-start.6 = (f32[2048]{0:T(1024)}, f32[2048]{0:T(1024)S(1)}, u32[]{:S(2)}) copy-start(f32[2048]{0:T(1024)S(1)} %fusion.83) | copy-start | bytes 24580
  525.7 34.5 %copy-start.9 = (f32[2048]{0:T(1024)S(1)}, f32[2048]{0:T(1024)}, u32[]{:S(2)}) copy-start(f32[2048]{0:T(1024)} %copy-done.8) | copy-start | bytes 24580
  572.5 54.4 %copy-start.3 = (f32[2048]{0:T(1024)S(1)}, f32[2048]{0:T(1024)}, u32[]{:S(2)}) copy-start(f32[2048]{0:T(1024)} %copy-done.2) | copy-start | bytes 24580
  664.6 0.7 copy-start.7
  664.6 369.0 %reduce-scatter.23.cloned.1.call-start = ((), (), s32[]{:S(2)}) async-start(), calls=%async_computation.13 | async-start | bytes 11827200
  702.7 435.1 %reduce-scatter.19.cloned.1.call-start = ((), (), s32[]{:S(2)}) async-start(), calls=%async_computation.11 | async-start | bytes 11827200
  734.3 0.7 copy-start.10
  734.3 1.9 copy-start.4
  734.4 522.6 %reduce-scatter.17.cloned.1.call-start = ((), (), s32[]{:S(2)}) async-start(), calls=%async_computation.10 | async-start | bytes 11827200
  806.3 514.6 %all-reduce.12.cloned.1.call-start = ((), (), s32[]{:S(2)}) async-start(), calls=%async_computation.14 | async-start | bytes 4341760 | tf_op jit(solution)/shard_map/psum | solution.py:31
  987.7 41.7 %collective-permute-start = (bf16[124,1280]{1,0:T(8,128)(2,1)S(1)}, bf16[124,1280]{1,0:T(8,128)(2,1)S(1)}, u32[]{:S(2)}, u32[]{:S(2)}) collective-permute-start(bf16[124,1280]{1,0:T(8,128)(2,1)S(1)} %slice.27), channel_id=1, source_target_pairs={{0,1},{1,2},{2,3},{3,4},{4,5},{5,6},{6,7},{7,8},{8,9},{9,10},{10,1... | collective-permute-start | bytes 952328
  992.2 38.4 %collective-permute-start.1 = (bf16[124,1280]{1,0:T(8,128)(2,1)S(1)}, bf16[124,1280]{1,0:T(8,128)(2,1)S(1)}, u32[]{:S(2)}, u32[]{:S(2)}) collective-permute-start(bf16[124,1280]{1,0:T(8,128)(2,1)S(1)} %slice.28), channel_id=1, source_target_pairs={{0,1},{1,2},{2,3},{3,4},{4,5},{5,6},{6,7},{7,8},{8,9},{9,10},{10,1... | collective-permute-start | bytes 952328
  1257.0 34.3 %copy-start.1 = (f32[2048]{0:T(1024)S(1)}, f32[2048]{0:T(1024)}, u32[]{:S(2)}) copy-start(f32[2048]{0:T(1024)} %copy-done) | copy-start | bytes 24580
  1257.0 34.3 %copy-start.5 = (f32[2048]{0:T(1024)S(1)}, f32[2048]{0:T(1024)}, u32[]{:S(2)}) copy-start(f32[2048]{0:T(1024)} %copy-done.2) | copy-start | bytes 24580
Sparse Core Ops, SparseCore 0:
  10.2 63.4 all-gather.12
  76.0 59.2 all-gather.14
  138.2 86.0 all-gather.16
  227.1 85.9 all-gather.20
  315.1 59.1 all-gather.22
  377.0 59.2 all-gather.18
  664.7 113.5 reduce-scatter.20
  782.2 236.0 reduce-scatter.22
  1022.2 115.4 reduce-scatter.18
  1141.4 115.5 reduce-scatter.16
  1260.3 60.5 all-reduce.11
where the time goes:
time: 1340 us; the launch traced here: 1330 us
  matrix products  643 us (48%)
  waiting for transfers between devices  445 us (33%)
  blocking collectives  151 us (11%)
  local copies, waits for them, and re-layouts  39.6 us (3%)
  other arithmetic  32 us (2%)
  between operations  15.1 us (1%)
    unnamed x17, waiting for transfers between devices  225 us
    dot_general x6, matrix products, layer(): up = jnp.dot(a, w['w_up'], preferred_element_type=jnp.float32)  223 us
    dot_general x6, matrix products, layer(): gate = jnp.dot(a, w['w_gate'], preferred_element_type=jnp.float32)  218 us
    all_gather x6, waiting for transfers between devices, fetched(): lax.all_gather(w[number], 's', axis=0, tiled=True)  210 us
    dot_general x5, matrix products, matmul(): jnp.dot(a, w, preferred_element_type=jnp.float32).astype(jnp.bfloat16)  203 us
    unnamed x1, blocking collectives  151 us
    unnamed x31, local copies, waits for them, and re-layouts  30.2 us
  transfers between devices with their start and end apart: 13, of which 9 were waited for; matrix products, arithmetic and copies ran while one was open for 47% of the time, Pallas kernels for 0%

commit v1 on v0

v1 whole, which is shorter than its diff:
```python
import functools

import jax
import jax.numpy as jnp
from jax import lax
from jax.experimental import pallas as pl
from jax.experimental.pallas import tpu as pltpu
from jax.sharding import PartitionSpec as P

BF, F32 = jnp.bfloat16, jnp.float32
MESH = pl.DeviceIdType.MESH
ANY = pl.BlockSpec(memory_space=pl.ANY)
T, D, F, FP = 2048, 1280, 4480, 4608
SIDE, CORES = 4, 2
HALF = FP // 2
EPS = 1e-6
VMEM = 62 * 2**20
NT = (((1,), (1,)), ((), ()))
TN = (((0,), (0,)), ((), ()))


class Me:
    def __init__(self, places):
        s = lax.axis_index("s")
        self.places = places
        self.x = lax.axis_index("r")
        self.k = lax.rem(s, CORES)
        self.z = lax.rem(lax.div(s, CORES), SIDE)
        self.y = lax.div(s, CORES * SIDE)

    def at(self, dx=0, dy=0, dz=0, dk=0):
        y, z, k = lax.rem(self.y + dy, SIDE), lax.rem(self.z + dz, SIDE), lax.rem(self.k + dk, CORES)
        return {"r": lax.rem(self.x + dx, self.places), "s": (y * SIDE + z) * CORES + k}


class Task:
    ins, outs, scratch, copies, locals_ = (), (), (), 0, 0

    def events(self, steps):
        return {}


def copy(refs, number, src, dst, to):
    return pltpu.make_async_remote_copy(
        src_ref=src, dst_ref=dst, send_sem=refs.send.at[number], recv_sem=refs.recv.at[number], device_id=to, device_id_type=MESH
    )


class Refs:
    pass


class Gather(Task):
    PER_COLOUR = 15

    def __init__(self, kinds, blocks, slots):
        self.kinds, self.slots = kinds, slots
        self.ins = [(b, pl.BlockSpec(b.shape, lambda *_: (0, 0))) for b in blocks]
        self.outs = []
        for kind, b in zip(kinds, blocks):
            lead = (SIDE, SIDE, CORES) if kind == "row" else (SIDE, SIDE)
            self.outs.append(jax.ShapeDtypeStruct(lead + b.shape, b.dtype))
        self.copies = 2 * self.PER_COLOUR * len(kinds)
        self.locals_ = len(kinds)
        self.peers = {(0, 1, 0, 0), (0, 3, 0, 0), (0, 0, 1, 0), (0, 0, 3, 0), (0, 0, 0, 1)}

    def part(self, kind, ref, me, y, z, colour, half):
        if kind == "row":
            start, size = ((0, 2304), (2304, 2304))[colour] if half is None else (2304 * colour + 1152 * half, 1152)
            return ref.at[y, z, me.k, :, pl.ds(start, size)]
        if half is None:
            start, size = ((0, 144), (144, 136))[colour]
        else:
            start, size = (((0, 72), (72, 72)), ((144, 72), (216, 64)))[colour][half]
        return ref.at[y, z, pl.ds(start, size), pl.ds(pl.multiple_of(me.k * (D // 2), 128), D // 2)]

    def own(self, kind, ref, me, colour):
        if kind == "row":
            return ref.at[:, pl.ds(2304 * colour, 2304)]
        start, size = ((0, 144), (144, 136))[colour]
        return ref.at[pl.ds(start, size), pl.ds(pl.multiple_of(me.k * (D // 2), 128), D // 2)]

    def place(self, me, refs, n):
        whole = refs.outs[n]
        dst = whole.at[me.y, me.z, me.k] if self.kinds[n] == "row" else whole.at[me.y, me.z]
        return pltpu.make_async_copy(refs.ins[n], dst, refs.local.at[n])

    def region(self, me, refs, n, colour, phase, along, half=None):
        on_y = (colour == 0) == (phase == 0)
        every = slice(None)
        y = along if on_y else (every if phase else me.y)
        z = (every if phase else me.z) if on_y else along
        return self.part(self.kinds[n], refs.outs[n], me, y, z, colour, half)

    def ring(self, me, refs, n, colour, phase, hop, turn):
        on_y = (colour == 0) == (phase == 0)
        place = me.y if on_y else me.z
        base = (2 * n + colour) * self.PER_COLOUR + 4 * phase + 2 * hop + turn
        step = 1 if turn == 0 else SIDE - 1
        to = me.at(dy=step) if on_y else me.at(dz=step)
        from_ = place if hop == 0 else lax.rem(place + SIDE - step, SIDE)
        dst = self.region(me, refs, n, colour, phase, from_, None if hop == 0 else turn)
        src = dst
        if hop == 0 and phase == 0:
            src = self.own(self.kinds[n], refs.ins[n], me, colour)
        return copy(refs, base, src, dst, to)

    def across(self, me, refs, n, colour, phase, away):
        on_y = (colour == 0) == (phase == 0)
        place = lax.rem((me.y if on_y else me.z) + away, SIDE)
        ref = self.region(me, refs, n, colour, phase, place)
        return copy(refs, (2 * n + colour) * self.PER_COLOUR + 8 + 3 * phase + away - 1, ref, ref, me.at(dk=1))

    def over(self):
        return [(n, c) for n in range(len(self.kinds)) for c in range(2)]

    def events(self, steps):
        def start(me, refs):
            for n, c in self.over():
                for turn in range(2):
                    self.ring(me, refs, n, c, 0, 0, turn).start()
            for n in range(len(self.kinds)):
                self.place(me, refs, n).start()

        def forward(phase):
            def run(me, refs):
                for turn in range(2):
                    for n, c in self.over():
                        self.ring(me, refs, n, c, phase, 0, turn).wait_recv()
                        self.ring(me, refs, n, c, phase, 1, turn).start()
                for n, c in self.over():
                    for away in (1, 3):
                        self.across(me, refs, n, c, phase, away).start()

            return run

        def second(me, refs):
            for n in range(len(self.kinds)):
                self.place(me, refs, n).wait()
            for n in range(len(self.kinds)):
                if self.kinds[n] == "row":
                    self.both(me, refs, n).start()
            for n, c in self.over():
                for turn in range(2):
                    self.ring(me, refs, n, c, 0, 1, turn).wait_recv()
                for turn in range(2):
                    self.ring(me, refs, n, c, 1, 0, turn).start()
                self.across(me, refs, n, c, 0, 2).start()

        def last(me, refs):
            for n, c in self.over():
                for turn in range(2):
                    self.ring(me, refs, n, c, 1, 1, turn).wait_recv()
                self.across(me, refs, n, c, 1, 2).start()

        def end(me, refs):
            for n, c in self.over():
                for phase in range(2):
                    for hop in range(2):
                        for turn in range(2):
                            self.ring(me, refs, n, c, phase, hop, turn).wait_send()
                    for away in (1, 2, 3):
                        self.across(me, refs, n, c, phase, away).wait()
            for n in range(len(self.kinds)):
                if self.kinds[n] == "row":
                    self.both(me, refs, n).wait()

        made = [start, forward(0), second, forward(1), last]
        found = {}
        for slot, run in zip(self.slots, made):
            found.setdefault(min(slot, steps - 1), []).append(run)
        found["end"] = [end]
        return found

    def both(self, me, refs, n):
        ref = refs.outs[n].at[me.y, me.z, me.k]
        return copy(refs, 2 * n * self.PER_COLOUR + 14, refs.ins[n], ref, me.at(dk=1))


class Sends(Task):
    def __init__(self, arrays, outs, peers, plan, copies, local=None):
        self.ins = [(a, ANY) for a in arrays]
        self.outs, self.peers, self.plan, self.copies, self.local = outs, peers, plan, copies, local
        self.locals_ = 1 if local else 0

    def made(self, me, refs):
        return [copy(refs, i, *entry) for i, entry in enumerate(self.plan(me, refs.ins, refs.outs))]

    def events(self, steps):
        def start(me, refs):
            for c in self.made(me, refs):
                c.start()
            if self.local:
                pltpu.make_async_copy(*self.local(me, refs.ins, refs.outs), refs.local.at[0]).start()

        def end(me, refs):
            for c in self.made(me, refs):
                c.wait()
            if self.local:
                pltpu.make_async_copy(*self.local(me, refs.ins, refs.outs), refs.local.at[0]).wait()

        return {0: [start], "end": [end]}


def colours(kind, ref, lead, colour):
    if kind == "row":
        return ref.at[(*lead, slice(None), pl.ds(1152 * colour, 1152))]
    start, size = ((0, 144), (144, 136))[colour]
    return ref.at[(*lead, pl.ds(start, size), slice(None))]


def colour_shape(kind, colour):
    return (80, 1152) if kind == "row" else ((144, 136)[colour], D // 2)


def first_sends(kind, terms):
    shape = [jax.ShapeDtypeStruct((SIDE - 1, SIDE, *colour_shape(kind, c)), BF) for c in range(2)]

    def plan(me, ins, outs):
        found = []
        for d in (1, 3, 2):
            y, z = lax.rem(me.y + d, SIDE), lax.rem(me.z + d, SIDE)
            found.append((colours(kind, ins[0], (y, slice(None)), 0), outs[0].at[d - 1], me.at(dy=d)))
            found.append((colours(kind, ins[0], (slice(None), z), 1), outs[1].at[d - 1], me.at(dz=d)))
        return found

    peers = {(0, d, 0, 0) for d in (1, 2, 3)} | {(0, 0, d, 0) for d in (1, 2, 3)}
    return Sends([terms], shape, peers, plan, 6)


def second_sends(kind, along_y, along_z):
    shape = [jax.ShapeDtypeStruct((SIDE - 1, *colour_shape(kind, c)), BF) for c in range(2)]

    def plan(me, ins, outs):
        found = []
        for d in (1, 3, 2):
            y, z = lax.rem(me.y + d, SIDE), lax.rem(me.z + d, SIDE)
            found.append((ins[0].at[z], outs[0].at[d - 1], me.at(dz=d)))
            found.append((ins[1].at[y], outs[1].at[d - 1], me.at(dy=d)))
        return found

    peers = {(0, d, 0, 0) for d in (1, 2, 3)} | {(0, 0, d, 0) for d in (1, 2, 3)}
    return Sends([along_y, along_z], shape, peers, plan, 6)


def third_sends(kind, places, total):
    rows, columns = (40, HALF) if kind == "row" else (144, D // 2)
    shape = [jax.ShapeDtypeStruct((places, CORES, rows, columns), BF)]

    def window(me, ref, k):
        start = (40 if kind == "row" else 136) * k
        return ref.at[pl.ds(pl.multiple_of(start, 8), rows), :]

    def plan(me, ins, outs):
        found = []
        for dk in (0, 1):
            for dx in range(places):
                if (dx, dk) != (0, 0):
                    src = window(me, ins[0], lax.rem(me.k + dk, CORES))
                    found.append((src, outs[0].at[me.x, me.k], me.at(dx=dx, dk=dk)))
        return found

    def local(me, ins, outs):
        return window(me, ins[0], me.k), outs[0].at[me.x, me.k]

    peers = {(dx, 0, 0, dk) for dx in range(places) for dk in (0, 1)} - {(0, 0, 0, 0)}
    return Sends([total], shape, peers, plan, 2 * places - 1, local)


def fused(name, number, places, steps, compute, ins, outs, scratch=(), tasks=(), flops=0, extra_peers=(), partner=0):
    lists = [ins, *[t.ins for t in tasks]]
    n_in = [len(l) for l in lists]
    out_lists = [outs, *[[(o, ANY) for o in t.outs] for t in tasks]]
    n_out = [len(l) for l in out_lists]
    peers = sorted(set(extra_peers).union(*[t.peers for t in tasks]) if tasks else set(extra_peers))
    sems = []
    for t in tasks:
        sems += [pltpu.SemaphoreType.DMA((t.copies,)), pltpu.SemaphoreType.DMA((t.copies,)), pltpu.SemaphoreType.DMA((max(t.locals_, 1),))]
    if partner:
        sems += [pltpu.SemaphoreType.DMA((partner,)), pltpu.SemaphoreType.DMA((partner,))]

    def kernel(*refs):
        refs = list(refs)
        take = lambda n: [refs.pop(0) for _ in range(n)]
        given = [take(n) for n in n_in]
        made = [take(n) for n in n_out]
        own = take(len(scratch))
        held = []
        for i, t in enumerate(tasks):
            r = Refs()
            r.ins, r.outs = given[1 + i], made[1 + i]
            r.send, r.recv, r.local = take(3)
            held.append(r)
        pair = take(2) if partner else None
        me = Me(places)
        step = pl.program_id(0)

        if peers:

            @pl.when(step == 0)
            def _():
                barrier = pltpu.get_barrier_semaphore()
                for dx, dy, dz, dk in peers:
                    pl.semaphore_signal(barrier, inc=1, device_id=me.at(dx, dy, dz, dk), device_id_type=MESH)
                pl.semaphore_wait(barrier, len(peers))

        plans = [t.events(steps) for t in tasks]
        for slot in range(steps):
            runs = [(run, r) for plan, r in zip(plans, held) for run in plan.get(slot, ())]
            if runs:

                @pl.when(step == slot)
                def _():
                    for run, r in runs:
                        run(me, r)

        compute(step, me, given[0], made[0], own, pair)

        ends = [(run, r) for plan, r in zip(plans, held) for run in plan.get("end", ())]
        if ends:

            @pl.when(step == steps - 1)
            def _():
                for run, r in ends:
                    run(me, r)

    arrays = [a for l in lists for a, _ in l]
    got = pl.pallas_call(
        kernel,
        grid=(steps,),
        in_specs=[s for l in lists for _, s in l],
        out_specs=[s for l in out_lists for _, s in l],
        out_shape=[o for l in out_lists for o, _ in l],
        scratch_shapes=[*scratch, *sems],
        name=name,
        cost_estimate=pl.CostEstimate(flops=int(flops), bytes_accessed=1 << 24, transcendentals=0),
        compiler_params=pltpu.CompilerParams(
            vmem_limit_bytes=VMEM,
            has_side_effects=bool(peers),
            **({"collective_id": number} if peers else {}),
        ),
    )(*arrays)
    got = list(got)
    return [[got.pop(0) for _ in range(n)] for n in n_out]


def whole(shape):
    return pl.BlockSpec(shape, lambda j: (0,) * len(shape))


def shaped(*shape, dtype=BF):
    return jax.ShapeDtypeStruct(shape, dtype)


def sigmoid(g):
    return 1.0 / (1.0 + jnp.exp(-g))


def chunks(total, size, body):
    size = min(size, total)

    def run(i, _):
        body(pl.ds(pl.multiple_of(i * size, size), size))
        return 0

    lax.fori_loop(0, total // size, run, 0)


def scale_of(wide):
    return lax.rsqrt(jnp.mean(wide * wide, -1, keepdims=True) + EPS)


def norm_kernel(number, places, x, tasks):
    steps = 8
    rows = T // steps

    def compute(step, me, ins, outs, own, pair):
        def body(r):
            wide = ins[0][r, :].astype(F32)
            outs[0][r, :] = (wide * scale_of(wide)).astype(BF)

        chunks(rows, 64, body)

    block = pl.BlockSpec((rows, D), lambda j: (j, 0))
    return fused("norm", number, places, steps, compute, [(x, block)], [(shaped(T, D), block)], tasks=tasks, flops=10 * T * D)


def gate_up_kernel(number, places, a, wg, wu, tasks, bn=512, mc=1024):
    def compute(step, me, ins, outs, own, pair):
        a, wg, wu = ins
        g_o, u_o, act_o = outs

        def body(r):
            rows = a[r, :]
            g = jnp.dot(rows, wg[...], preferred_element_type=F32)
            u = jnp.dot(rows, wu[...], preferred_element_type=F32)
            g_o[r, :] = g
            u_o[r, :] = u
            act_o[r, :] = (g * sigmoid(g) * u).astype(BF)

        chunks(T, mc, body)

    block = pl.BlockSpec((T, bn), lambda j: (0, j))
    w = pl.BlockSpec((D, bn), lambda j: (0, j))
    return fused(
        "gate_up", number, places, FP // bn, compute, [(a, whole((T, D))), (wg, w), (wu, w)],
        [(shaped(T, FP, dtype=F32), block), (shaped(T, FP, dtype=F32), block), (shaped(T, FP), block)], tasks=tasks, flops=4 * T * D * FP,
    )


def down_kernel(number, places, act, wd, h, tasks, bk=512, mc=512):
    steps = FP // bk
    tail = F - (steps - 1) * bk

    def compute(step, me, ins, outs, own, pair):
        act, wd, h = ins
        h_o, a_o = outs
        (acc,) = own

        @pl.when(step == 0)
        def _():
            def zero(r):
                acc[r, :] = jnp.zeros((min(128, acc.shape[0]), D), F32)

            chunks(T, 128, zero)

        def add(depth):
            def body(r):
                acc[r, :] = acc[r, :] + jnp.dot(act[r, :depth], wd[:depth, :], preferred_element_type=F32)

            chunks(T, mc, body)

        @pl.when(step < steps - 1)
        def _():
            add(bk)

        @pl.when(step == steps - 1)
        def _():
            add(tail)

            def finish(r):
                y = (h[r, :].astype(F32) + acc[r, :].astype(BF).astype(F32)).astype(BF)
                h_o[r, :] = y
                wide = y.astype(F32)
                a_o[r, :] = (wide * scale_of(wide)).astype(BF)

            chunks(T, 64, finish)

    return fused(
        "down", number, places, steps, compute,
        [(act, pl.BlockSpec((T, bk), lambda j: (0, j))), (wd, pl.BlockSpec((bk, D), lambda j: (j, 0))), (h, whole((T, D)))],
        [(shaped(T, D), whole((T, D))), (shaped(T, D), whole((T, D)))], [pltpu.VMEM((T, D), F32)], tasks=tasks, flops=2 * T * D * FP,
    )


def by_act_kernel(number, places, by_h, wd, g, u, tasks, bn=512, mc=512):
    def compute(step, me, ins, outs, own, pair):
        by_h, wd, g, u = ins
        dg_o, du_o = outs
        inside = lax.broadcasted_iota(jnp.int32, (min(mc, T), bn), 1) + step * bn < F

        def body(r):
            d = lax.dot_general(by_h[r, :], wd[...], NT, preferred_element_type=F32)
            d = jnp.where(inside, d, 0.0).astype(BF).astype(F32)
            gate, up = g[r, :], u[r, :]
            s = sigmoid(gate)
            gs = gate * s
            du_o[r, :] = (d * gs).astype(BF)
            dg_o[r, :] = (d * up * (s + gs * (1.0 - s))).astype(BF)

        chunks(T, mc, body)

    block = pl.BlockSpec((T, bn), lambda j: (0, j))
    return fused(
        "by_act", number, places, FP // bn, compute,
        [(by_h, whole((T, D))), (wd, pl.BlockSpec((bn, D), lambda j: (j, 0))), (g, block), (u, block)],
        [(shaped(T, FP), block), (shaped(T, FP), block)], tasks=tasks, flops=2 * T * D * FP,
    )


def by_row_kernel(number, places, a, dg, tasks, bn=768, mc=640):
    n = HALF // bn

    def columns(j):
        k = lax.rem(lax.axis_index("s"), CORES)
        return (0, jnp.where(j < n, (1 - k) * n + j, k * n + j - n))

    def compute(step, me, ins, outs, own, pair):
        a, dg = ins
        sum_o, wide_o = outs
        mine, theirs = own

        def send(i):
            return pltpu.make_async_remote_copy(
                src_ref=mine.at[i], dst_ref=theirs.at[i], send_sem=pair[0].at[i], recv_sem=pair[1].at[i], device_id=me.at(dk=1), device_id_type=MESH
            )

        def dot(r):
            return lax.dot_general(a[:, r], dg[...], TN, preferred_element_type=F32)

        for i in range(n):

            @pl.when(step == i + 1)
            def _():
                send(i).start()

        @pl.when(step < n)
        def _():
            def body(r):
                mine[step, r, :] = dot(r).astype(BF)

            chunks(D, mc, body)

        for i in range(n):

            @pl.when(step == n + i)
            def _():
                send(i).wait_recv()

        @pl.when(step >= n)
        def _():
            def body(r):
                total = dot(r) + theirs[step - n, r, :].astype(F32)
                wide_o[r, :] = total
                sum_o[r, :] = total.astype(BF)

            chunks(D, mc, body)

        @pl.when(step == 2 * n - 1)
        def _():
            for i in range(n):
                send(i).wait_send()

    out = pl.BlockSpec((D, bn), lambda j: (0, jnp.maximum(j - n, 0)))
    return fused(
        "by_row", number, places, 2 * n, compute, [(a, whole((T, D))), (dg, pl.BlockSpec((T, bn), columns))],
        [(shaped(D, HALF), out), (shaped(D, HALF, dtype=F32), out)],
        [pltpu.VMEM((n, D, bn), BF), pltpu.VMEM((n, D, bn), BF)], tasks=tasks, flops=2 * T * D * FP, extra_peers={(0, 0, 0, 1)}, partner=n,
    )


def by_down_kernel(number, places, act, by_h, tasks, bm=768, mc=384):
    n = FP // bm
    width = D // 2

    def compute(step, me, ins, outs, own, pair):
        act, by_h = ins
        sum_o, wide_o = outs
        mine, theirs = own
        half = jnp.where(step < n, 1 - me.k, me.k)
        columns = pl.ds(pl.multiple_of(half * width, 128), width)

        def send(i):
            return pltpu.make_async_remote_copy(
                src_ref=mine.at[i], dst_ref=theirs.at[i], send_sem=pair[0].at[i], recv_sem=pair[1].at[i], device_id=me.at(dk=1), device_id_type=MESH
            )

        def dot(r):
            return lax.dot_general(act[:, r], by_h[:, columns], TN, preferred_element_type=F32)

        for i in range(n):

            @pl.when(step == i + 1)
            def _():
                send(i).start()

        @pl.when(step < n)
        def _():
            def body(r):
                mine[step, r, :] = dot(r).astype(BF)

            chunks(bm, mc, body)

        for i in range(n):

            @pl.when(step == n + i)
            def _():
                send(i).wait_recv()

        @pl.when(step >= n)
        def _():
            def body(r):
                total = dot(r) + theirs[step - n, r, :].astype(F32)
                wide_o[r, :] = total
                sum_o[r, :] = total.astype(BF)

            chunks(bm, mc, body)

        @pl.when(step == 2 * n - 1)
        def _():
            for i in range(n):
                send(i).wait_send()

    out = pl.BlockSpec((bm, width), lambda j: (jnp.maximum(j - n, 0), 0))
    return fused(
        "by_down", number, places, 2 * n, compute,
        [(act, pl.BlockSpec((T, bm), lambda j: (0, lax.rem(j, n)))), (by_h, whole((T, D)))],
        [(shaped(F, width), out), (shaped(F, width, dtype=F32), out)],
        [pltpu.VMEM((n, bm, width), BF), pltpu.VMEM((n, bm, width), BF)], tasks=tasks, flops=2 * T * D * FP, extra_peers={(0, 0, 0, 1)}, partner=n,
    )


def by_input_kernel(number, places, dg, du, wg, wu, h, by_h, tasks, part=0, parts=1, bk=512, mc=1024):
    steps = FP // bk
    rows = T // parts

    def compute(step, me, ins, outs, own, pair):
        dg, du, wg, wu, h, by_h = ins
        (acc,) = own

        @pl.when(step == 0)
        def _():
            def zero(r):
                acc[r, :] = jnp.zeros((min(128, acc.shape[0]), D), F32)

            chunks(rows, 128, zero)

        def body(r):
            p = lax.dot_general(dg[r, :], wg[...], NT, preferred_element_type=F32)
            p = p + lax.dot_general(du[r, :], wu[...], NT, preferred_element_type=F32)
            acc[r, :] = acc[r, :] + p

        chunks(rows, mc, body)

        @pl.when(step == steps - 1)
        def _():
            def finish(r):
                by_a = acc[r, :].astype(BF).astype(F32)
                wide = h[r, :].astype(F32)
                scale = scale_of(wide)
                along = jnp.sum(by_a * wide, -1, keepdims=True)
                by_wide = by_a * scale - wide * (scale * scale * scale * along * (1.0 / D))
                outs[0][r, :] = (by_h[r, :].astype(F32) + by_wide.astype(BF).astype(F32)).astype(BF)

            chunks(rows, 64, finish)

    tokens = pl.BlockSpec((rows, bk), lambda j: (part, j))
    w = pl.BlockSpec((D, bk), lambda j: (0, j))
    block = pl.BlockSpec((rows, D), lambda j: (part, 0))
    return fused(
        "by_input", number, places, steps, compute,
        [(dg, tokens), (du, tokens), (wg, w), (wu, w), (h, block), (by_h, block)],
        [(shaped(rows, D), whole((rows, D)))], [pltpu.VMEM((rows, D), F32)], tasks=tasks, flops=4 * rows * D * FP,
    )


def sends_kernel(number, places, tasks):
    def compute(step, me, ins, outs, own, pair):
        pass

    return fused("sends", number, places, 1, compute, [], [], tasks=tasks)


class Sum:
    def __init__(self, kind, me, places, made):
        self.kind, self.me, self.places = kind, me, places
        self.narrow, self.wide = (m.reshape(SIDE, SIDE, m.shape[0] // SIDE**2, m.shape[1]) for m in made)

    def first(self):
        return first_sends(self.kind, self.narrow)

    def after_first(self, got):
        y, z, _, _ = self.me
        c = lambda n: (slice(None), slice(None), slice(1152 * n, 1152 * n + 1152)) if self.kind == "row" else (slice(None), slice(*((0, 144), (144, 280))[n]))
        own_y = lax.dynamic_index_in_dim(self.wide, y, 0, keepdims=False)[c(0)]
        own_z = lax.dynamic_index_in_dim(self.wide, z, 1, keepdims=False)[c(1)]
        self.sums = [own + got[n][0].astype(F32) + got[n][1].astype(F32) + got[n][2].astype(F32) for n, own in enumerate((own_y, own_z))]
        self.narrow = [s.astype(BF) for s in self.sums]

    def second(self):
        return second_sends(self.kind, *self.narrow)

    def after_second(self, got):
        y, z, _, _ = self.me
        own = [lax.dynamic_index_in_dim(s, i, 0, keepdims=False) for s, i in zip(self.sums, (z, y))]
        sums = [o + g[0].astype(F32) + g[1].astype(F32) + g[2].astype(F32) for o, g in zip(own, got)]
        self.total = jnp.concatenate(sums, 1 if self.kind == "row" else 0).astype(BF)

    def third(self):
        return third_sends(self.kind, self.places, self.total)

    def done(self, got):
        terms = got[0].astype(F32)
        total = terms[0]
        for i in range(1, self.places):
            total = total + terms[i]
        if self.kind == "row":
            return jnp.concatenate([total[0], total[1]], 1)[:, :F].astype(BF)
        k = self.me[2]
        rows = F // SIDE**2 // CORES
        both = jnp.concatenate([total[0], total[1]], 1)
        return jnp.where(k == 0, both[:rows], both[144 - rows :]).astype(BF)


def solution(mesh):
    places = mesh.shape["r"]

    def step(x, dy, w_gate, w_up, w_down):
        x, dy = x[0], dy[0]
        s = lax.axis_index("s")
        k = s % CORES
        me = (s // (CORES * SIDE), (s // CORES) % SIDE, k, lax.axis_index("r"))
        n_s = SIDE * SIDE * CORES
        gate = [jnp.pad(w_gate[i], ((0, 0), (0, FP - F))) for i in range(2)]
        up = [jnp.pad(w_up[i], ((0, 0), (0, FP - F))) for i in range(2)]
        other = lax.ppermute(w_down, "s", [(i, i ^ 1) for i in range(n_s)])
        down = jnp.where(k == 0, jnp.concatenate([w_down, other], 1), jnp.concatenate([other, w_down], 1))
        rows = lambda m: m.reshape(D, FP)
        chip = lambda m: m.reshape(F, D)
        add = functools.partial(Sum, me=me, places=places)

        (a0,), (g0, u0) = norm_kernel(0, places, x, [Gather(["row", "row"], [gate[0], up[0]], (0, 1, 2, 4, 6))])
        wg0, wu0 = rows(g0), rows(u0)
        (gate0, up0, act0), (d0, g1) = gate_up_kernel(1, places, a0, wg0, wu0, [Gather(["chip", "row"], [down[0], gate[1]], (0, 1, 2, 6, 8))])
        wd0, wg1 = chip(d0), rows(g1)
        (h1, a1), (u1,) = down_kernel(2, places, act0, wd0, x, [Gather(["row"], [up[1]], (0, 1, 2, 6, 8))])
        wu1 = rows(u1)
        (gate1, up1, act1), (d1,) = gate_up_kernel(3, places, a1, wg1, wu1, [Gather(["chip"], [down[1]], (0, 1, 2, 5, 7))])
        wd1 = chip(d1)

        ((dg1, du1),) = by_act_kernel(4, places, dy, wd1, gate1, up1, [])
        (made,) = by_down_kernel(5, places, act1, dy, [])
        sum_d1 = add("chip", made=made)
        made, got = by_row_kernel(6, places, a1, dg1, [sum_d1.first()])
        sum_d1.after_first(got)
        sum_g1 = add("row", made=made)
        (by_h1,), got, more = by_input_kernel(7, places, dg1, du1, wg1, wu1, h1, dy, [sum_g1.first(), sum_d1.second()])
        sum_g1.after_first(got)
        sum_d1.after_second(more)
        made, got, more = by_down_kernel(8, places, act0, by_h1, [sum_d1.third(), sum_g1.second()])
        out_d1 = sum_d1.done(got)
        sum_g1.after_second(more)
        sum_d0 = add("chip", made=made)
        made, got = by_row_kernel(9, places, a1, du1, [sum_d0.first()])
        sum_d0.after_first(got)
        sum_u1 = add("row", made=made)
        (dg0, du0), got, more, last = by_act_kernel(10, places, by_h1, wd0, gate0, up0, [sum_u1.first(), sum_g1.third(), sum_d0.second()])
        sum_u1.after_first(got)
        out_g1 = sum_g1.done(more)
        sum_d0.after_second(last)
        made, got, more = by_row_kernel(11, places, a0, dg0, [sum_u1.second(), sum_d0.third()])
        sum_u1.after_second(got)
        out_d0 = sum_d0.done(more)
        sum_g0 = add("row", made=made)
        made, got, more = by_row_kernel(12, places, a0, du0, [sum_g0.first(), sum_u1.third()])
        sum_g0.after_first(got)
        out_u1 = sum_u1.done(more)
        sum_u0 = add("row", made=made)
        (low,), got, more = by_input_kernel(13, places, dg0, du0, wg0, wu0, x, by_h1, [sum_u0.first(), sum_g0.second()], 0, 2)
        sum_u0.after_first(got)
        sum_g0.after_second(more)
        (high,), got, more = by_input_kernel(14, places, dg0, du0, wg0, wu0, x, by_h1, [sum_u0.second(), sum_g0.third()], 1, 2)
        sum_u0.after_second(got)
        out_g0 = sum_g0.done(more)
        _, got = sends_kernel(15, places, [sum_u0.third()])
        out_u0 = sum_u0.done(got)
        by_x = jnp.concatenate([low, high], 0)
        return by_x[None], jnp.stack([out_g0, out_g1]), jnp.stack([out_u0, out_u1]), jnp.stack([out_d0, out_d1])

    states, cut = P(("rep", "r", "s"), None, None), P(None, "s", None)
    return jax.shard_map(
        step,
        mesh=mesh,
        in_specs=(states, states) + (cut,) * 3,
        out_specs=(states,) + (P("rep", "s", None),) * 3,
        check_vma=False,
    )
```

time: 1340 us -> 938 us (0.70)
  Pallas kernels: 0 us -> 817 us
  matrix products: 643 us -> 0 us
  waiting for transfers between devices: 445 us -> 0.01 us
  blocking collectives: 151 us -> 0 us
  other arithmetic: 32 us -> 52.9 us
  local copies, waits for them, and re-layouts: 39.6 us -> 57.4 us
  between operations: 15.1 us -> 1.55 us
    pallas_call x0 -> x16, Pallas kernels: none -> 817 us  [fused(): pl.pallas_call(kernel, grid=(steps,), in_specs=[s for l in lists for _, s...]
    dot_general x17 -> x0, matrix products: 643 us -> none  [the longest x6 223 us: layer(): up = jnp.dot(a, w['w_up'], preferred_element_type=jnp.float32)]
    unnamed x17 -> x0, waiting for transfers between devices: 225 us -> none
    all_gather x6 -> x0, waiting for transfers between devices: 210 us -> none  [fetched(): lax.all_gather(w[number], 's', axis=0, tiled=True)]
    unnamed x1 -> x0, blocking collectives: 151 us -> none
    squeeze x0 -> x19, local copies, waits for them, and re-layouts: none -> 42.6 us  [the longest x5 19.7 us: after_first(): own_y = lax.dynamic_index_in_dim(self.wide, y, 0, keepdims=False)[c(0)]]
    convert_element_type x0 -> x18, other arithmetic: none -> 27.9 us  [the longest x12 25.2 us: after_first(): self.narrow = [s.astype(BF) for s in self.sums]]
    unnamed x31 -> x58, local copies, waits for them, and re-layouts: 30.2 us -> 11.7 us
  transfers between devices with their start and end apart: 13 -> 1, of which waited for: 9 -> 0; matrix products, arithmetic and copies ran while one was open for 47% -> 1% of each run, Pallas kernels for 0% -> 8%
where the time goes in v1:
time: 938 us; the launch traced here: 930 us
  Pallas kernels  817 us (87%)
  local copies, waits for them, and re-layouts  57.4 us (6%)
  other arithmetic  52.9 us (6%)
    pallas_call x16, Pallas kernels, fused(): pl.pallas_call(kernel, grid=(steps,), in_specs=[s for l in lists for _, s...  817 us
    convert_element_type x12, other arithmetic, after_first(): self.narrow = [s.astype(BF) for s in self.sums]  25.2 us
    squeeze x5, local copies, waits for them, and re-layouts, after_first(): own_y = lax.dynamic_index_in_dim(self.wide, y, 0, keepdims=False)[c(0)]  19.7 us
    squeeze x5, local copies, waits for them, and re-layouts, after_first(): own_z = lax.dynamic_index_in_dim(self.wide, z, 1, keepdims=False)[c(1)]  19.6 us
  transfers between devices with their start and end apart: 1, of which 0 were waited for; matrix products, arithmetic and copies ran while one was open for 1% of the time, Pallas kernels for 8%

profile of v1, /device:TPU:1, one launch (start us, length us, event | category | flops | bytes accessed | tf_op | source)
XLA Modules:
  0.0 930.1 jit_solution(14076247294510059287)
XLA Ops:
  0.6 1.4 collective-permute-start
  2.1 1.3 copy.19
  7.6 74.3 %norm.1 = (bf16[2048,1280]{1,0:T(8,128)(2,1)}, bf16[4,4,2,40,4608]{4,3,2,1,0:T(8,128)(2,1)}, bf16[4,4,2,40,4608]{4,3,2,1,0:T(8,128)(2,1)}) custom-call(bf16[2048,1280]{1,0:T(8,128)(2,1)} %bitcast.281, bf16[40,4608]{1,0:T(8,128)(2,1)} %pad.13.refs_1_, bf16[40,4608]{1,0:T(8,128)(2,1)} %pad.14.refs_2_), custom_call_target="tpu_custom_call" | custom-call | flops 26214400 | bytes 16777216 | tf_op jit(solution)/shard_map/norm/pallas_call | solution.py:328
  83.7 82.1 %gate_up.2 = (f32[2048,4608]{1,0:T(8,128)}, f32[2048,4608]{1,0:T(8,128)}, bf16[2048,4608]{1,0:T(8,128)(2,1)}, bf16[4,4,280,1280]{3,2,1,0:T(8,128)(2,1)}, bf16[4,4,2,40,4608]{4,3,2,1,0:T(8,128)(2,1)}) custom-call(bf16[2048,1280]{1,0:T(8,128)(2,1)} %get-tuple-element.67.refs_0_, bf16[1280,4608]{1,0:T(8,128)(2,1)} %bitcast.297, bf16[1280,4608]{1,0:T(8,128)(2,1)} %bitcast.300, ...), custom_call_target="tpu_custom_call" | custom-call | flops 48318382080 | bytes 16777216 | tf_op jit(solution)/shard_map/gate_up/pallas_call | solution.py:328
  165.9 52.3 %down.1 = (bf16[2048,1280]{1,0:T(8,128)(2,1)}, bf16[2048,1280]{1,0:T(8,128)(2,1)}, bf16[4,4,2,40,4608]{4,3,2,1,0:T(8,128)(2,1)}) custom-call(bf16[2048,4608]{1,0:T(8,128)(2,1)} %get-tuple-element.70.refs_0_, bf16[4480,1280]{1,0:T(8,128)(2,1)} %bitcast.274, bf16[2048,1280]{1,0:T(8,128)(2,1)} %bitcast.282, bf16[40,4608]{1,0:T(8,128)(2,1)} %pad.16.refs_3_), custom_call_target="tpu_custom_call" | custom-call | flops 24159191040 | bytes 16777216 | tf_op jit(solution)/shard_map/down/pallas_call | solution.py:328
  218.2 67.9 %gate_up.3 = (f32[2048,4608]{1,0:T(8,128)}, f32[2048,4608]{1,0:T(8,128)}, bf16[2048,4608]{1,0:T(8,128)(2,1)}, bf16[4,4,280,1280]{3,2,1,0:T(8,128)(2,1)}) custom-call(bf16[2048,1280]{1,0:T(8,128)(2,1)} %get-tuple-element.72.refs_0_, bf16[1280,4608]{1,0:T(8,128)(2,1)} %bitcast.303, bf16[1280,4608]{1,0:T(8,128)(2,1)} %bitcast.305, ...), custom_call_target="tpu_custom_call" | custom-call | flops 48318382080 | bytes 16777216 | tf_op jit(solution)/shard_map/gate_up/pallas_call | solution.py:328
  286.1 43.6 %by_down.2 = (bf16[4480,640]{1,0:T(8,128)(2,1)}, f32[4480,640]{1,0:T(8,128)}) custom-call(bf16[2048,4608]{1,0:T(8,128)(2,1)} %get-tuple-element.81.refs_0_, bf16[2048,1280]{1,0:T(8,128)(2,1)} %bitcast.278), custom_call_target="tpu_custom_call" | custom-call | flops 24159191040 | bytes 16777216 | tf_op jit(solution)/shard_map/by_down/pallas_call | solution.py:328
  329.7 3.6 dynamic-slice_bitcast_fusion.10
  333.4 3.5 dynamic-slice_bitcast_fusion.11
  336.9 53.1 %by_act.2 = (bf16[2048,4608]{1,0:T(8,128)(2,1)}, bf16[2048,4608]{1,0:T(8,128)(2,1)}) custom-call(bf16[2048,1280]{1,0:T(8,128)(2,1)} %bitcast.279, bf16[4480,1280]{1,0:T(8,128)(2,1)} %bitcast.276, f32[2048,4608]{1,0:T(8,128)} %get-tuple-element.76.refs_2_, f32[2048,4608]{1,0:T(8,128)} %get-tuple-element.77.refs_3_), custom_call_target="tpu_custom_call" | custom-call | flops 24159191040 | bytes 16777216 | tf_op jit(solution)/shard_map/by_act/pallas_call | solution.py:328
  390.0 41.9 %by_row.4 = (bf16[1280,2304]{1,0:T(8,128)(2,1)}, f32[1280,2304]{1,0:T(8,128)}, bf16[3,4,144,640]{3,2,1,0:T(8,128)(2,1)}, bf16[3,4,136,640]{3,2,1,0:T(8,128)(2,1)}) custom-call(bf16[2048,1280]{1,0:T(8,128)(2,1)} %get-tuple-element.72.refs_0_, bf16[2048,4608]{1,0:T(8,128)(2,1)} %get-tuple-element.78.refs_1_.refs_0_, bf16[4,4,280,640]{3,2,1,0:T(8,128)(2,1)} %bitcast.311), custom_call_target="tpu_custom_call" | custom-call | flops 24159191040 | bytes 16777216 | tf_op jit(solution)/shard_map/by_row/pallas_call | solution.py:328
  431.9 3.7 dynamic-slice_bitcast_fusion.6
  435.6 3.9 dynamic-slice_bitcast_fusion.7
  439.5 3.1 fusion.70
  442.6 1.3 fusion.72
  443.9 70.6 %by_input.3 = (bf16[2048,1280]{1,0:T(8,128)(2,1)}, bf16[3,4,80,1152]{3,2,1,0:T(8,128)(2,1)}, bf16[3,4,80,1152]{3,2,1,0:T(8,128)(2,1)}, bf16[3,144,640]{2,1,0:T(8,128)(2,1)}, bf16[3,136,640]{2,1,0:T(8,128)(2,1)}) custom-call(bf16[2048,4608]{1,0:T(8,128)(2,1)} %get-tuple-element.78.refs_1_.refs_0_, bf16[2048,4608]{1,0:T(8,128)(2,1)} %get-tuple-element.79.refs_1_, ...), custom_call_target="tpu_custom_call" | custom-call | flops 48318382080 | bytes 16777216 | tf_op jit(solution)/shard_map/by_input/pallas_call | solution.py:328
  514.5 1.4 fusion.48
  517.9 2.8 fusion.68
  521.0 1.7 fusion.66
  522.6 45.9 %by_down.3 = (bf16[4480,640]{1,0:T(8,128)(2,1)}, f32[4480,640]{1,0:T(8,128)}, bf16[4,2,144,640]{3,2,1,0:T(8,128)(2,1)}, bf16[3,80,1152]{2,1,0:T(8,128)(2,1)}, bf16[3,80,1152]{2,1,0:T(8,128)(2,1)}) custom-call(bf16[2048,4608]{1,0:T(8,128)(2,1)} %get-tuple-element.70.refs_0_, bf16[2048,1280]{1,0:T(8,128)(2,1)} %get-tuple-element.87.refs_1_.refs_0_.refs_5_, ...), custom_call_target="tpu_custom_call" | custom-call | flops 24159191040 | bytes 16777216 | tf_op jit(solution)/shard_map/by_down/pallas_call | solution.py:328
  568.6 3.7 dynamic-slice_bitcast_fusion.8
  572.2 3.6 dynamic-slice_bitcast_fusion.9
  575.8 41.4 %by_row.5 = (bf16[1280,2304]{1,0:T(8,128)(2,1)}, f32[1280,2304]{1,0:T(8,128)}, bf16[3,4,144,640]{3,2,1,0:T(8,128)(2,1)}, bf16[3,4,136,640]{3,2,1,0:T(8,128)(2,1)}) custom-call(bf16[2048,1280]{1,0:T(8,128)(2,1)} %get-tuple-element.72.refs_0_, bf16[2048,4608]{1,0:T(8,128)(2,1)} %get-tuple-element.79.refs_1_, bf16[4,4,280,640]{3,2,1,0:T(8,128)(2,1)} %bitcast.310), custom_call_target="tpu_custom_call" | custom-call | flops 24159191040 | bytes 16777216 | tf_op jit(solution)/shard_map/by_row/pallas_call | solution.py:328
  617.1 3.7 dynamic-slice_bitcast_fusion.4
  620.9 3.9 dynamic-slice_bitcast_fusion.5
  624.8 1.2 fusion.40
  628.7 3.0 fusion.62
  631.7 55.9 %by_act.3 = (bf16[2048,4608]{1,0:T(8,128)(2,1)}, bf16[2048,4608]{1,0:T(8,128)(2,1)}, bf16[3,4,80,1152]{3,2,1,0:T(8,128)(2,1)}, bf16[3,4,80,1152]{3,2,1,0:T(8,128...) custom-call(bf16[2048,1280]{1,0:T(8,128)(2,1)} %get-tuple-element.87.refs_1_.re, ...), custom_call_target="tpu_custom_call" | custom-call | flops 24159191040 | bytes 16777216 | tf_op jit(solution)/shard_map/by_act/pallas_call | solution.py:328
  687.6 1.4 fusion.49
  691.0 2.8 fusion.60
  694.1 1.7 fusion.58
  695.7 36.9 %by_row.6 = (bf16[1280,2304]{1,0:T(8,128)(2,1)}, f32[1280,2304]{1,0:T(8,128)}, bf16[3,80,1152]{2,1,0:T(8,128)(2,1)}, bf16[3,80,1152]{2,1,0:T(8,128)(2,1)}, bf16[4,2,144,640]{3,2,1,0:T(8,128)(2,1)}) custom-call(bf16[2048,1280]{1,0:T(8,128)(2,1)} %get-tuple-element.67.refs_0_, bf16[2048,4608]{1,0:T(8,128)(2,1)} %get-tuple-element.102.refs_1_.refs_0_, ...), custom_call_target="tpu_custom_call" | custom-call | flops 24159191040 | bytes 16777216 | tf_op jit(solution)/shard_map/by_row/pallas_call | solution.py:328
  732.7 1.3 fusion.43
  735.9 42.1 %by_row.7 = (bf16[1280,2304]{1,0:T(8,128)(2,1)}, f32[1280,2304]{1,0:T(8,128)}, bf16[3,4,80,1152]{3,2,1,0:T(8,128)(2,1)}, bf16[3,4,80,1152]{3,2,1,0:T(8,128)(2,1)}, bf16[4,2,40,2304]{3,2,1,0:T(8,128)(2,1)}) custom-call(bf16[2048,1280]{1,0:T(8,128)(2,1)} %get-tuple-element.67.refs_0_, bf16[2048,4608]{1,0:T(8,128)(2,1)} %get-tuple-element.103.refs_1_, ...), custom_call_target="tpu_custom_call" | custom-call | flops 24159191040 | bytes 16777216 | tf_op jit(solution)/shard_map/by_row/pallas_call | solution.py:328
  778.0 4.8 dynamic-slice_bitcast_fusion
  782.8 4.9 dynamic-slice_bitcast_fusion.1
  791.6 1.4 copy.29
  796.9 1.8 fusion.56
  798.6 48.5 %by_input.4 = (bf16[1024,1280]{1,0:T(8,128)(2,1)}, bf16[3,4,80,1152]{3,2,1,0:T(8,128)(2,1)}, bf16[3,4,80,1152]{3,2,1,0:T(8,128)(2,1)}, bf16[3,80,1152]{2,1,0:T(8,128)(2,1)}, bf16[3,80,1152]{2,1,0:T(8,128)(2,1)}) custom-call(bf16[2048,4608]{1,0:T(8,128)(2,1)} %get-tuple-element.102.refs_1_.refs_0_, bf16[2048,4608]{1,0:T(8,128)(2,1)} %get-tuple-element.103.refs_1_, ...), custom_call_target="tpu_custom_call" | custom-call | flops 24159191040 | bytes 16777216 | tf_op jit(solution)/shard_map/by_input/pallas_call | solution.py:328
  847.2 1.3 fusion.45
  848.5 1.3 fusion.44
  850.6 3.0 fusion.50
  853.9 1.7 fusion.52
  855.6 40.0 %by_input.5 = (bf16[1024,1280]{1,0:T(8,128)(2,1)}, bf16[3,80,1152]{2,1,0:T(8,128)(2,1)}, bf16[3,80,1152]{2,1,0:T(8,128)(2,1)}, bf16[4,2,40,2304]{3,2,1,0:T(8,128)(2,1)}) custom-call(bf16[2048,4608]{1,0:T(8,128)(2,1)} %get-tuple-element.102.refs_1_.refs_0_, bf16[2048,4608]{1,0:T(8,128)(2,1)} %get-tuple-element.103.refs_1_, bf16[1280,4608]{1,0:T(8,128)(2,1)} %bitcast.299, ...), custom_call_target="tpu_custom_call" | custom-call | flops 24159191040 | bytes 16777216 | tf_op jit(solution)/shard_map/by_input/pallas_call | solution.py:328
  896.8 1.3 fusion.46
  898.9 20.4 %sends.1 = bf16[4,2,40,2304]{3,2,1,0:T(8,128)(2,1)} custom-call(bf16[80,2304]{1,0:T(8,128)(2,1)} %pad_maximum_fusion.8.refs_0_), custom_call_target="tpu_custom_call" | custom-call | bytes 16777216 | tf_op jit(solution)/shard_map/sends/pallas_call | solution.py:328
  919.2 1.6 convert_element_type.557
  925.0 2.7 maximum_bitcast_fusion
  (104 shorter events, 32.0 us)
Async XLA Ops:
  0.6 81.3 %collective-permute-start = (bf16[2,140,1280]{2,0,1:T(2,128)(2,1)}, bf16[2,140,1280]{2,0,1:T(2,128)(2,1)S(1)}, u32[]{:S(2)}, u32[]{:S(2)}) collective-permute-start(bf16[2,140,1280]{2,0,1:T(2,128)(2,1)} %param.9), channel_id=1, source_target_pairs={{0,1},{1,0},{2,3},{3,2},{4,5},{5,4},{6,7},{7,6},{8,9},{9,8},{10,11... | collective-permute-start | bytes 2150408 | tf_op jit(solution)/shard_map/ppermute | solution.py:706
  2.1 4.0 copy-start.25
  435.6 3.9 copy-start.18
  439.5 3.1 copy-start.4
  439.5 3.2 copy-start.16
  514.5 3.4 copy-start.14
  517.9 2.8 copy-start.3
  517.9 3.1 copy-start.11
  620.9 3.9 copy-start.27
  620.9 5.1 copy-start.26
  620.9 6.0 copy-start.15
  624.8 2.1 copy-start.5
  626.9 1.9 copy-start.17
  687.6 3.4 copy-start.12
  691.0 2.8 copy-start.2
  691.0 3.1 copy-start.10
  782.8 4.9 copy-start.20
  788.0 1.4 copy-start.19
  789.6 1.4 copy-start.22
  791.3 1.7 copy-start.21
  793.3 1.7 copy-start.9
  795.0 1.9 copy-start.8
  847.2 3.4 copy-start.1
  850.6 3.0 copy-start
  850.6 3.3 copy-start.13
  920.9 1.4 copy-start.23
  922.2 0.9 copy-start.24
  922.5 1.8 copy-start.6
  922.5 2.5 copy-start.7
